TPU v7x, 32 devices: a whole 2x2x4 slice. The times are simulated.
32 devices in a mesh: dp: 8 (over z, x), mp: 4 (over y, core).
Axes of the slice: x: 2, y: 2, z: 4, core: 2. Of those that a mesh axis runs over, the one named last changes fastest.
Arguments:
- patches: bfloat16 [4096, 2048], P('dp'), may hold values from -6 to 6
- cotangent: bfloat16 [4096, 8192], P('dp', 'mp'), may hold values from -0.09375 to 0.09375
- weight: float32 [2048, 8192], P('dp', 'mp'), may hold values from -0.125 to 0.125
- accum: float32 [2048, 8192], P('dp', 'mp'), may hold values from 0.1 to 4
Outputs:
- new_weight: float32 [2048, 8192], P(('dp', 'mp'))
- new_accum: float32 [2048, 8192], P(('dp', 'mp'))
- weight_copy: bfloat16 [2048, 8192], P(None, 'mp')
All inputs are finite; a program needn't handle non-finite values.
Results may differ from a plain program's by a relative error of at most 0.001.
Values may be sent and summed in bfloat16 or wider, within the bound.
A program may use at most 192 MiB of HBM per device.

v0:
```python
import jax
import jax.numpy as jnp
from jax import lax
from jax.sharding import PartitionSpec as P

learning_rate = 0.02


def adagrad(accum, weight, grad):
    summed = accum + grad * grad
    return (summed, weight - learning_rate * grad * lax.rsqrt(summed))


def shards(patches, cotangent, weight, accum):
    patch_block = lax.all_to_all(patches, "dp", split_axis=1, concat_axis=0, tiled=True)
    grad_block = jnp.einsum(
        "tr,tf->rf",
        patch_block,
        lax.all_gather(cotangent, "dp", axis=0, tiled=True),
        preferred_element_type=jnp.float32,
    )
    accum_block, weight_block = adagrad(accum, weight, grad_block)
    weight_copy = lax.all_gather(weight_block.astype(jnp.bfloat16), "dp", axis=0, tiled=True)
    new_accum, new_weight = (
        lax.all_to_all(accum_block, "mp", split_axis=0, concat_axis=1, tiled=True),
        lax.all_to_all(weight_block, "mp", split_axis=0, concat_axis=1, tiled=True),
    )
    return (new_weight, new_accum, weight_copy)


def solution(mesh):
    return jax.shard_map(
        shards,
        mesh=mesh,
        in_specs=(P("dp", None), P("dp", "mp"), P("dp", "mp"), P("dp", "mp")),
        out_specs=(P(("dp", "mp"), None), P(("dp", "mp"), None), P(None, "mp")),
        check_vma=False,
    )
```

profile of v0, /device:TPU:0, one launch (start us, length us, event | category | flops | bytes accessed | tf_op | source)
XLA Modules:
  0.0 430.2 jit_solution(2336489553796141500)
XLA Ops:
  7.2 0.0 all-gather.3.cloned.1.call-start
  7.2 0.7 all-gather.3.cloned.1.call-update
  7.9 0.0 all-gather.5.cloned.1.call-start
  7.9 2.9 copy.11
  10.8 107.2 %all_to_all.57 = bf16[512,8,256]{0,2,1:T(8,128)(2,1)} all-to-all(bf16[512,8,256]{0,2,1:T(8,128)(2,1)S(1)} %bitcast.18), channel_id=1, replica_groups=mesh['dp'=8,'mp'=4] {'dp'}, dimensions={1} | all-to-all | bytes 4194304 | tf_op jit(solution)/shard_map/all_to_all | solution.py:15
  118.0 2.8 copy.12
  120.9 158.3 %all-gather.3.cloned.1.call-done = bf16[4096,2048]{1,0:T(8,128)(2,1)} async-done(((bf16[512,2048]{1,0:T(8,128)(2,1)}), bf16[4096,2048]{1,0:T(8,128)(2,1)}) %all-gather.3.cloned.1.call-update) | async-done | bytes 16777232 | tf_op jit(solution)/shard_map/all_gather | solution.py:19
  279.1 12.9 %fusion = (bf16[256,2048]{1,0:T(8,128)(2,1)}, f32[256,2048]{1,0:T(8,128)}, f32[256,2048]{1,0:T(8,128)}) fusion(f32[256,2048]{1,0:T(8,128)} %param.6, f32[256,2048]{1,0:T(8,128)} %param.7, bf16[4096,256]{1,0:T(8,128)(2,1)S(1)} %bitcast.13, bf16[4096,2048]{1,0:T(8,128)(2,1)} %all-gather.3.cloned.1.call-done), kind=kOutput, calls=%fused_computation.2 | convolution fusion | flops 4298113024 | bytes 28311552 | tf_op jit(solution)/shard_map/tr,tf->rf/dot_general | solution.py:16
  292.0 0.0 all-gather.5.cloned.1.call-update
  292.1 30.2 %all_to_all.58 = f32[4,64,2048]{2,1,0:T(8,128)} all-to-all(f32[4,64,2048]{2,1,0:T(8,128)} %bitcast.14), channel_id=1, replica_groups=mesh['dp'=8,'mp'=4] {'mp'}, dimensions={0} | all-to-all | bytes 4194304 | tf_op jit(solution)/shard_map/all_to_all | solution.py:26
  322.2 3.6 all-to-all-start.2
  325.8 3.1 copy.15
  329.0 22.5 %all-to-all-done.2 = f32[4,64,2048]{2,1,0:T(8,128)S(1)} async-done(((f32[4,64,2048]{2,1,0:T(8,128)}), f32[4,64,2048]{2,1,0:T(8,128)S(1)}, u32[]{:S(2)}, u32[]{:S(2)}) %all-to-all-start.2) | async-done | bytes 2097184 | tf_op jit(solution)/shard_map/all_to_all | solution.py:25
  351.5 1.5 copy.16
  352.9 61.9 %all-gather.5.cloned.1.call-done = bf16[2048,2048]{1,0:T(8,128)(2,1)} async-done(((bf16[256,2048]{1,0:T(8,128)(2,1)}), bf16[2048,2048]{1,0:T(8,128)(2,1)}) %all-gather.5.cloned.1.call-update) | async-done | bytes 8388624 | tf_op jit(solution)/shard_map/all_gather | solution.py:23
  414.9 8.4 %copy.18 = bf16[2048,2048]{1,0:T(8,128)(2,1)} copy(bf16[2048,2048]{1,0:T(8,128)(2,1)} %all-gather.5.cloned.1.call-done) | data formatting | bytes 16777216
Async XLA Ops:
  7.2 272.0 %all-gather.3.cloned.1.call-start = ((), (), s32[]{:S(2)}) async-start(), calls=%async_computation.3 | async-start | bytes 18874368 | tf_op jit(solution)/shard_map/all_gather | solution.py:19
  7.9 407.0 %all-gather.5.cloned.1.call-start = ((), (), s32[]{:S(2)}) async-start(), calls=%async_computation.4 | async-start | bytes 9437184 | tf_op jit(solution)/shard_map/all_gather | solution.py:23
  322.2 29.3 %all-to-all-start.2 = ((f32[4,64,2048]{2,1,0:T(8,128)}), f32[4,64,2048]{2,1,0:T(8,128)S(1)}, u32[]{:S(2)}, u32[]{:S(2)}) async-start(f32[4,64,2048]{2,1,0:T(8,128)} %bitcast.5), calls=%async_computation.2 | async-start | bytes 4194304 | tf_op jit(solution)/shard_map/all_to_all | solution.py:25
Sparse Core Ops, SparseCore 0:
  10.1 268.9 all-gather.2
  292.2 122.6 all-gather.4
where the time goes:
time: 431 us; the launch traced here: 430 us
  waiting for transfers between devices  243 us (56%)
  blocking collectives  137 us (32%)
  local copies, waits for them, and re-layouts  18.8 us (4%)
  between operations  14.1 us (3%)
  matrix products  12.9 us (3%)
    all_gather x1, waiting for transfers between devices, shards(): lax.all_gather(cotangent, 'dp', axis=0, tiled=True)  158 us
    all_to_all x1, blocking collectives, shards(): lax.all_to_all(patches, 'dp', split_axis=1, concat_axis=0, tiled=True)  107 us
    all_gather x1, waiting for transfers between devices, shards(): lax.all_gather(weight_block.astype(jnp.bfloat16), 'dp', axis=0, tiled=True)  61.9 us
    all_to_all x1, blocking collectives, shards(): lax.all_to_all(weight_block, 'mp', split_axis=0, concat_axis=1, tiled=True)  30.2 us
    all_to_all x1, waiting for transfers between devices, shards(): lax.all_to_all(accum_block, 'mp', split_axis=0, concat_axis=1, tiled=True)  22.5 us
    dot_general x1, matrix products, shards(): jnp.einsum('tr,tf->rf', patch_block, lax.all_gather(cotangent, 'dp', axis...  12.9 us
    unnamed x2, local copies, waits for them, and re-layouts  11.3 us
  transfers between devices with their start and end apart: 3, of which 3 were waited for; matrix products, arithmetic and copies ran while one was open for 2% of the time, Pallas kernels for 0%

commit v1 on v0

--- a/solution.py
+++ b/solution.py
@@ -4,6 +4,29 @@
 from jax.sharding import PartitionSpec as P
 
 learning_rate = 0.02
+
+
+def cut_along(value, dim, length):
+    shape = value.shape
+    pieces = value.reshape(*shape[:dim], length, shape[dim] // length, *shape[dim + 1 :])
+    return jnp.moveaxis(pieces, dim, 0)
+
+
+def in_order(parts, dim):
+    shape = list(parts.shape[1:])
+    shape[dim] *= parts.shape[0]
+    return jnp.moveaxis(parts, 0, dim).reshape(shape)
+
+
+def rotated_exchange(x, axis, split_dim, concat_dim):
+    peers, here = (lax.axis_size(axis), lax.axis_index(axis))
+    blocks = cut_along(x, split_dim, peers)
+    outs = [blocks[here]]
+    for step in range(1, peers):
+        sent = blocks[(here + step) % peers]
+        outs.append(lax.ppermute(sent, axis, [(i, (i + step) % peers) for i in range(peers)]))
+    blocks = jnp.stack(outs)[(here - jnp.arange(peers)) % peers]
+    return in_order(blocks, concat_dim)
 
 
 def adagrad(accum, weight, grad):
@@ -22,7 +45,7 @@
     accum_block, weight_block = adagrad(accum, weight, grad_block)
     weight_copy = lax.all_gather(weight_block.astype(jnp.bfloat16), "dp", axis=0, tiled=True)
     new_accum, new_weight = (
-        lax.all_to_all(accum_block, "mp", split_axis=0, concat_axis=1, tiled=True),
+        rotated_exchange(accum_block, "mp", 0, 1),
         lax.all_to_all(weight_block, "mp", split_axis=0, concat_axis=1, tiled=True),
     )
     return (new_weight, new_accum, weight_copy)

time: 431 us -> 431 us (level)
  blocking collectives: 137 us -> 107 us
  waiting for transfers between devices: 243 us -> 266 us
    ppermute x0 -> x3, waiting for transfers between devices: none -> 45.6 us  [rotated_exchange(): lax.ppermute(sent, axis, [(i, (i + step) % peers) for i in range(peers)])]
    all_to_all x1 -> x0, blocking collectives: 30.2 us -> none  [shards(): lax.all_to_all(weight_block, 'mp', split_axis=0, concat_axis=1, tiled=True)]
    all_to_all x1, waiting for transfers between devices: 22.5 us -> 0.01 us  [shards(): lax.all_to_all(weight_block, 'mp', split_axis=0, concat_axis=1, tiled=True)]
    unnamed x2 -> x4, local copies, waits for them, and re-layouts: 11.3 us -> 11.3 us
  transfers between devices with their start and end apart: 3 -> 6, of which waited for: 3 -> 4; matrix products, arithmetic and copies ran while one was open for 2% -> 3% of each run, Pallas kernels for 0% -> 0%
where the time goes in v1:
time: 431 us; the launch traced here: 430 us
  waiting for transfers between devices  266 us (62%)
  blocking collectives  107 us (25%)
  local copies, waits for them, and re-layouts  22.7 us (5%)
  between operations  14.1 us (3%)
  matrix products  12.9 us (3%)
  starting transfers between devices  6.91 us (2%)
    all_gather x1, waiting for transfers between devices, shards(): lax.all_gather(cotangent, 'dp', axis=0, tiled=True)  158 us
    all_to_all x1, blocking collectives, shards(): lax.all_to_all(patches, 'dp', split_axis=1, concat_axis=0, tiled=True)  107 us
    all_gather x1, waiting for transfers between devices, shards(): lax.all_gather(weight_block.astype(jnp.bfloat16), 'dp', axis=0, tiled=True)  61.6 us
    ppermute x3, waiting for transfers between devices, rotated_exchange(): lax.ppermute(sent, axis, [(i, (i + step) % peers) for i in range(peers)])  45.6 us
    dot_general x1, matrix products, shards(): jnp.einsum('tr,tf->rf', patch_block, lax.all_gather(cotangent, 'dp', axis...  12.9 us
    unnamed x4, local copies, waits for them, and re-layouts  11.3 us
  transfers between devices with their start and end apart: 6, of which 4 were waited for; matrix products, arithmetic and copies ran while one was open for 3% of the time, Pallas kernels for 0%

profile of v1, /device:TPU:0, one launch (start us, length us, event | category | flops | bytes accessed | tf_op | source)
XLA Modules:
  0.0 430.1 jit_solution(9466205077020851405)
XLA Ops:
  7.2 0.0 all-gather.3.cloned.1.call-start
  7.2 0.7 all-gather.3.cloned.1.call-update
  7.9 0.0 all-gather.5.cloned.1.call-start
  7.9 2.9 copy.11
  10.8 107.2 %all_to_all.38 = bf16[512,8,256]{0,2,1:T(8,128)(2,1)} all-to-all(bf16[512,8,256]{0,2,1:T(8,128)(2,1)S(1)} %bitcast.29), channel_id=1, replica_groups=mesh['dp'=8,'mp'=4] {'dp'}, dimensions={1} | all-to-all | bytes 4194304 | tf_op jit(solution)/shard_map/all_to_all | solution.py:38
  118.0 2.8 copy.12
  120.9 158.3 %all-gather.3.cloned.1.call-done = bf16[4096,2048]{1,0:T(8,128)(2,1)} async-done(((bf16[512,2048]{1,0:T(8,128)(2,1)}), bf16[4096,2048]{1,0:T(8,128)(2,1)}) %all-gather.3.cloned.1.call-update) | async-done | bytes 16777232 | tf_op jit(solution)/shard_map/all_gather | solution.py:42
  279.1 12.9 %fusion.2 = (bf16[256,2048]{1,0:T(8,128)(2,1)}, f32[256,2048]{1,0:T(8,128)}, f32[256,2048]{1,0:T(8,128)}) fusion(f32[256,2048]{1,0:T(8,128)} %param.6, f32[256,2048]{1,0:T(8,128)} %param.7, bf16[4096,256]{1,0:T(8,128)(2,1)S(1)} %bitcast.24, bf16[4096,2048]{1,0:T(8,128)(2,1)} %all-gather.3.cloned.1.call-done), kind=kOutput, calls=%fused_computation.15 | convolution fusion | flops 4298113024 | bytes 28311552 | tf_op jit(solution)/shard_map/tr,tf->rf/dot_general | solution.py:39
  292.0 0.0 all-gather.5.cloned.1.call-update
  292.1 0.0 copy-start
  292.1 4.6 %all-to-all-start.1 = ((f32[4,64,2048]{2,1,0:T(8,128)}), f32[4,64,2048]{2,1,0:T(8,128)}, u32[]{:S(2)}, u32[]{:S(2)}) async-start(f32[4,64,2048]{2,1,0:T(8,128)} %bitcast.25), calls=%async_computation.1 | async-start | bytes 4194304 | tf_op jit(solution)/shard_map/all_to_all | solution.py:49
  296.8 0.2 constant_dynamic-slice_fusion
  297.0 1.7 collective-permute-start.2
  298.7 0.4 collective-permute-start.1
  299.1 0.1 collective-permute-start
  299.2 32.5 %collective-permute-done.2 = f32[64,2048]{1,0:T(8,128)S(1)} collective-permute-done((f32[64,2048]{1,0:T(8,128)S(1)}, f32[64,2048]{1,0:T(8,128)S(1)}, u32[]{:S(2)}, u32[]{:S(2)}) %collective-permute-start.2) | collective-permute-done | bytes 524320 | tf_op jit(solution)/shard_map/ppermute | solution.py:27
  331.7 13.1 %collective-permute-done.1 = f32[64,2048]{1,0:T(8,128)S(1)} collective-permute-done((f32[64,2048]{1,0:T(8,128)S(1)}, f32[64,2048]{1,0:T(8,128)S(1)}, u32[]{:S(2)}, u32[]{:S(2)}) %collective-permute-start.1) | collective-permute-done | bytes 524320 | tf_op jit(solution)/shard_map/ppermute | solution.py:27
  344.8 0.0 collective-permute-done
  344.8 0.2 pad_maximum_fusion
  345.0 2.0 gather_fusion
  347.0 3.1 copy.16
  350.2 3.1 copy.15
  353.3 61.6 %all-gather.5.cloned.1.call-done = bf16[2048,2048]{1,0:T(8,128)(2,1)} async-done(((bf16[256,2048]{1,0:T(8,128)(2,1)}), bf16[2048,2048]{1,0:T(8,128)(2,1)}) %all-gather.5.cloned.1.call-update) | async-done | bytes 8388624 | tf_op jit(solution)/shard_map/all_gather | solution.py:46
  414.9 8.4 %copy.18 = bf16[2048,2048]{1,0:T(8,128)(2,1)} copy(bf16[2048,2048]{1,0:T(8,128)(2,1)} %all-gather.5.cloned.1.call-done) | data formatting | bytes 16777216
  (4 shorter events, 0.0 us)
Async XLA Ops:
  7.2 272.0 %all-gather.3.cloned.1.call-start = ((), (), s32[]{:S(2)}) async-start(), calls=%async_computation.2 | async-start | bytes 18874368 | tf_op jit(solution)/shard_map/all_gather | solution.py:42
  7.9 407.0 %all-gather.5.cloned.1.call-start = ((), (), s32[]{:S(2)}) async-start(), calls=%async_computation.3 | async-start | bytes 9437184 | tf_op jit(solution)/shard_map/all_gather | solution.py:46
  292.1 4.7 %copy-start = (f32[256,2048]{1,0:T(8,128)S(1)}, f32[256,2048]{1,0:T(8,128)}, u32[]{:S(2)}) copy-start(f32[256,2048]{1,0:T(8,128)} %get-tuple-element.5) | copy-start | bytes 6291460
  292.1 58.1 %all-to-all-start.1 = ((f32[4,64,2048]{2,1,0:T(8,128)}), f32[4,64,2048]{2,1,0:T(8,128)}, u32[]{:S(2)}, u32[]{:S(2)}) async-start(f32[4,64,2048]{2,1,0:T(8,128)} %bitcast.25), calls=%async_computation.1 | async-start | bytes 4194304 | tf_op jit(solution)/shard_map/all_to_all | solution.py:49
  297.0 34.7 %collective-permute-start.2 = (f32[64,2048]{1,0:T(8,128)S(1)}, f32[64,2048]{1,0:T(8,128)S(1)}, u32[]{:S(2)}, u32[]{:S(2)}) collective-permute-start(f32[64,2048]{1,0:T(8,128)S(1)} %get-tuple-element.7), channel_id=1, source_target_pairs={{0,3},{1,0},{2,1},{3,2},{4,7},{5,4},{6,5},{7,6},{8,11},{9,8},{10,9... | collective-permute-start | bytes 1572872 | tf_op jit(solution)/shard_map/ppermute | solution.py:27
  298.7 46.1 %collective-permute-start.1 = (f32[64,2048]{1,0:T(8,128)S(1)}, f32[64,2048]{1,0:T(8,128)S(1)}, u32[]{:S(2)}, u32[]{:S(2)}) collective-permute-start(f32[64,2048]{1,0:T(8,128)S(1)} %get-tuple-element.8), channel_id=1, source_target_pairs={{0,2},{1,3},{2,0},{3,1},{4,6},{5,7},{6,4},{7,5},{8,10},{9,11},{10,... | collective-permute-start | bytes 1572872 | tf_op jit(solution)/shard_map/ppermute | solution.py:27
  299.1 45.7 %collective-permute-start = (f32[64,2048]{1,0:T(8,128)S(1)}, f32[64,2048]{1,0:T(8,128)S(1)}, u32[]{:S(2)}, u32[]{:S(2)}) collective-permute-start(f32[64,2048]{1,0:T(8,128)S(1)} %get-tuple-element.9), channel_id=1, source_target_pairs={{0,1},{1,2},{2,3},{3,0},{4,5},{5,6},{6,7},{7,4},{8,9},{9,10},{10,1... | collective-permute-start | bytes 1572872 | tf_op jit(solution)/shard_map/ppermute | solution.py:27
Sparse Core Ops, SparseCore 0:
  10.1 268.9 all-gather.2
  292.2 122.6 all-gather.4
